TPU v7x, 32 devices: a whole 2x2x4 slice. The times are simulated.
32 devices in a mesh: dp: 2 (over x), m1: 4 (over z), m2: 4 (over y, core).
Axes of the slice: x: 2, y: 2, z: 4, core: 2. Of those that a mesh axis runs over, the one named last changes fastest.
Arguments:
- x: bfloat16 [16, 256, 6144], P('dp', None, 'm1'), parts along dimension 0
- ln_scale: float32 [6144], replicated
- qn_scale: float32 [128], replicated
- kn_scale: float32 [128], replicated
- w_qkv: bfloat16 [6144, 3, 6144], P('m1', None, 'm2')
- w_up: bfloat16 [6144, 24576], P('m1', 'm2')
- b_up: float32 [24576], P('m2')
- w_o: bfloat16 [6144, 6144], P('m2', 'm1')
- w_down: bfloat16 [24576, 6144], P('m2', 'm1')
- b_out: float32 [6144], P('m1')
Outputs:
- output: bfloat16 [16, 256, 6144], P('dp', None, 'm1'), parts along dimension 0
There are 2 independent parts. A program takes and returns all parts, laid end to end along the dimension named above; an argument that names none is the same for every part.
All inputs are finite; a program needn't handle non-finite values.
Results may differ from a plain program's by a relative error of at most 0.0107519.
Values are sent between devices in bfloat16 or wider.
A program may use at most 1 GiB of HBM per device.

v0:
```python
import functools

import jax
import jax.numpy as jnp
from jax import lax
from jax.experimental import pallas as pl
from jax.experimental.pallas import tpu as pltpu
from jax.sharding import PartitionSpec as P

LN_EPS = 1e-6
MESH = pl.DeviceIdType.MESH
LANES = 128
AHEAD = 2


def xors(value):
    return (value, value + 1 - 2 * lax.rem(value, 2), value + 2 - 4 * lax.div(value, 2), 3 - value)


def ds(start, size):
    return pl.ds(pl.multiple_of(start, size if size < LANES else LANES), size)


def rows_at(start, size):
    return pl.ds(pl.multiple_of(start, 8), size)


def rcopy(src, dst, send_sem, recv_sem, device):
    return pltpu.make_async_remote_copy(src_ref=src, dst_ref=dst, send_sem=send_sem, recv_sem=recv_sem, device_id=device, device_id_type=MESH)


def dot(lhs, rhs):
    return jnp.dot(lhs, rhs, preferred_element_type=jnp.float32)


def head_norm(values, scale):
    mean = jnp.mean(values, axis=-1, keepdims=True)
    centered = values - mean
    variance = jnp.mean(centered * centered, axis=-1, keepdims=True)
    return (centered * lax.rsqrt(variance + LN_EPS) * scale).astype(jnp.bfloat16)


def kernel(sizes, x, lns, qns, kns, wq, wu, bu, wo, wd, bo,
           out, u, w1, w2, ra,
           xg, ubl, zq, h, rhs, lhs, w2b, pa, po, rav, ss, rb, rc, ud, rd,
           xs, xr, w1s, w1r, f1s, f1r, us, ur, w2s, w2r, f2s, f2r,
           as_, ar, bs, br, cs, cr, dsm, drm, es, er, fr, own_sem, rhs_sem, lhs_sem, ub_sem, w2b_sem, rav_sem):
    batch, patches, dim, qw, uw = sizes
    tokens = batch * patches
    rows = tokens // 4
    block = rows // 2
    half = dim // 2
    total = 4 * dim
    nub = uw // qw
    nc = dim // LANES
    wide = 4 * LANES
    heads = qw // LANES
    ln_rows = min(64, rows)

    g, i, j = lax.axis_index('dp'), lax.axis_index('m1'), lax.axis_index('m2')
    ip, jp = xors(i), xors(j)
    jy, jc = lax.div(j, 2), lax.rem(j, 2)
    mid = lax.div(lax.rem(i + 1, 4), 2)
    peers1 = ((0, ip[1]), (2 - mid, ip[3] + mid * (ip[2] - ip[3])), (1 + mid, ip[2] + mid * (ip[3] - ip[2])))

    barrier = pltpu.get_barrier_semaphore()
    peers = [{'m1': ip[e]} for e in (1, 2, 3)] + [{'m2': jp[e]} for e in (1, 2, 3)] + [{'dp': 1 - g}]
    for peer in peers:
        pl.semaphore_signal(barrier, inc=1, device_id=peer, device_id_type=MESH)
    pl.semaphore_wait(barrier, len(peers))

    mine = rows_at(j * rows, rows)
    x_far = rcopy(x.at[mine, :], xg.at[i], xs.at[0], xr.at[0], {'m1': ip[2]})
    x_near = rcopy(x.at[mine, :], xg.at[i], xs.at[1], xr.at[1], {'m1': ip[1]})
    x_own = pltpu.make_async_copy(x.at[mine, :], xg.at[i], own_sem.at[0])
    x_far.start()
    x_near.start()
    x_own.start()
    x_far_in = rcopy(xg.at[ip[2]], xg.at[ip[2]], xs.at[0], xr.at[0], {'m1': ip[2]})
    x_far_in.wait_recv()
    x_fwd = rcopy(xg.at[ip[2]], xg.at[ip[2]], xs.at[2], xr.at[2], {'m1': ip[1]})
    x_fwd.start()

    def z1(b, e):
        t = ip[e]
        if b < 3:
            src = wq.at[b, rows_at(g * half, half), ds(t * qw, qw)]
        else:
            src = wu.at[rows_at(g * half, half), ds(t * uw + (b - 3) * qw, qw)]
        return rcopy(src, w1.at[b, rows_at(i * dim + g * half, half), :], w1s.at[0], w1r.at[b, e - 1], {'m1': t})

    def piece1(b, k, s):
        part = w1.at[b, rows_at(s * dim + g * half, half), :]
        return (rcopy(part, part, w1s.at[0], w1r.at[b, k], {'m1': s}), rcopy(part, part, f1s.at[0], f1r.at[b], {'dp': 1 - g}))

    def forward1(b):
        for k, s in peers1:
            arrival, swap = piece1(b, k, s)
            arrival.wait_recv()
            swap.start()

    def swapped1(b):
        part = w1.at[b, 0:3 * half, :]
        return rcopy(part, part, f1s.at[0], f1r.at[b], {'dp': 1 - g})

    def issue1(b):
        for e in (2, 3, 1):
            z1(b, e).start()

    issue1(0)
    issue1(1)

    qh, uh = qw // 2, uw // 2

    def z2(c, e):
        t = ip[e]
        cols, to = ds(c * LANES, LANES), ds(i * LANES, LANES)
        return [rcopy(wd.at[rows_at(t * uw + g * uh, uh), cols], w2.at[c, g, qh:qh + uh, to], w2s.at[0], w2r.at[c, e - 1], {'m1': t}),
                rcopy(wo.at[rows_at(t * qw + g * qh, qh), cols], w2.at[c, g, 0:qh, to], w2s.at[0], w2r.at[c, e - 1], {'m1': t})]

    def issue2(c):
        for e in (2, 3, 1):
            for copy in z2(c, e):
                copy.start()

    def forward2(c):
        for k, s in peers1:
            part = w2.at[c, g, :, ds(s * LANES, LANES)]
            rcopy(part, part, w2s.at[0], w2r.at[c, k], {'m1': s}).wait_recv()
            rcopy(part, part, f2s.at[0], f2r.at[c], {'dp': 1 - g}).start()

    def next2(c):
        forward2(c)

        @pl.when(c + AHEAD < nc)
        def _():
            issue2(c + AHEAD)

    x_own.wait()
    rcopy(xg.at[ip[1]], xg.at[ip[1]], xs.at[1], xr.at[1], {'m1': ip[1]}).wait_recv()
    rcopy(xg.at[ip[3]], xg.at[ip[3]], xs.at[2], xr.at[2], {'m1': ip[1]}).wait_recv()

    def u_out(r, slot):
        return pltpu.make_async_copy(ubl.at[slot], u.at[rows_at(j * rows + r * ln_rows, ln_rows), :], ub_sem.at[slot])

    @pl.loop(0, rows // ln_rows)
    def _(r):
        slot = lax.rem(r, 2)

        @pl.when(r >= 2)
        def _():
            u_out(r - 2, slot).wait()
        at = rows_at(r * ln_rows, ln_rows)
        parts = [xg[s, at, :].astype(jnp.float32) for s in range(4)]
        mean = sum(jnp.sum(part, axis=-1, keepdims=True) for part in parts) / total
        parts = [part - mean for part in parts]
        variance = sum(jnp.sum(part * part, axis=-1, keepdims=True) for part in parts) / total
        inverse = lax.rsqrt(variance + LN_EPS)
        for s in range(4):
            cols = slice(s * dim, (s + 1) * dim)
            ubl[slot, :, cols] = (parts[s] * inverse * lns[:, cols]).astype(jnp.bfloat16)
        u_out(r, slot).start()

    for r in range(max(0, rows // ln_rows - 2), rows // ln_rows):
        u_out(r, r % 2).wait()

    def u_rows(q):
        return u.at[rows_at(q * rows, rows), :]

    u_far = rcopy(u_rows(j), u_rows(j), us.at[0], ur.at[0], {'m2': jp[2]})
    u_near = rcopy(u_rows(j), u_rows(j), us.at[1], ur.at[1], {'m2': jp[1]})
    u_far.start()
    u_near.start()
    for b in range(4):
        forward1(b)
        issue1(b + 2)
    rcopy(u_rows(jp[2]), u_rows(jp[2]), us.at[0], ur.at[0], {'m2': jp[2]}).wait_recv()
    u_fwd = rcopy(u_rows(jp[2]), u_rows(jp[2]), us.at[2], ur.at[2], {'m2': jp[1]})
    u_fwd.start()
    rcopy(u_rows(jp[1]), u_rows(jp[1]), us.at[1], ur.at[1], {'m2': jp[1]}).wait_recv()
    rcopy(u_rows(jp[3]), u_rows(jp[3]), us.at[2], ur.at[2], {'m2': jp[1]}).wait_recv()

    def lhs_in(m, slot):
        return pltpu.make_async_copy(u.at[rows_at(m * block, block), :], lhs.at[slot], lhs_sem.at[slot])

    def product1(b, own, store):
        swapped1(b).wait_recv()
        loads = [pltpu.make_async_copy(own, rhs.at[rows_at(i * dim, dim), :], rhs_sem.at[0])]
        for e in (1, 2, 3):
            at = rows_at(ip[e] * dim, dim)
            loads.append(pltpu.make_async_copy(w1.at[b, at, :], rhs.at[at, :], rhs_sem.at[e]))
        for load in loads:
            load.start()
        lhs_in(0, 0).start()
        for load in loads:
            load.wait()

        @pl.loop(0, tokens // block)
        def _(m):
            slot = lax.rem(m, 2)
            lhs_in(m, slot).wait()

            @pl.when(m + 1 < tokens // block)
            def _():
                lhs_in(m + 1, 1 - slot).start()
            store(rows_at(m * block, block), dot(lhs[slot], rhs[...]))

    @pl.loop(0, 3)
    def _(b):
        def store(at, value):
            zq[b, at, :] = value.astype(jnp.bfloat16)
        product1(b, wq.at[b, :, ds(i * qw, qw)], store)

        @pl.when(b == 1)
        def _():
            forward1(4)
            issue1(6)

    @pl.loop(0, batch)
    def _(n):
        at = rows_at(n * patches, patches)
        for head in range(heads):
            cols = slice(head * LANES, (head + 1) * LANES)
            query = head_norm(zq[0, at, cols].astype(jnp.float32), qns[...])
            key = head_norm(zq[1, at, cols].astype(jnp.float32), kns[...])
            scores = lax.dot_general(query, key, (((1,), (1,)), ((), ())), preferred_element_type=jnp.float32) * LANES ** -0.5
            scores = jnp.exp(scores - jnp.max(scores, axis=-1, keepdims=True))
            probs = (scores / jnp.sum(scores, axis=-1, keepdims=True)).astype(jnp.bfloat16)
            h[at, cols] = dot(probs, zq[2, at, cols]).astype(jnp.bfloat16)

    forward1(5)
    for c in range(AHEAD // 2):
        issue2(c)

    @pl.loop(0, nub)
    def _(b):
        def store(at, value):
            value = value.astype(jnp.bfloat16).astype(jnp.float32) + bu[:, ds(i * uw + b * qw, qw)]
            value = 0.5 * value * (1.0 + lax.erf(value * 2.0 ** -0.5))
            h[at, ds(qw + b * qw, qw)] = value.astype(jnp.bfloat16)
        product1(b + 3, wu.at[:, ds(i * uw + b * qw, qw)], store)

        @pl.when(b == 1)
        def _():
            forward1(6)
            for c in range(AHEAD // 2, AHEAD):
                issue2(c)

        @pl.when(b == 2)
        def _():
            next2(0)

        @pl.when(b == 3)
        def _():
            next2(1)

    def quarter(yy, core):
        return (2 * yy + core) * rows

    def send_a(c, yy):
        return rcopy(pa.at[lax.rem(c, 2), yy], ra.at[c, yy], as_.at[lax.rem(c, 2)], ar.at[c], {'m2': jp[1]})

    def all_a(c):
        return rcopy(pa.at[lax.rem(c, 2)], ra.at[c], as_.at[lax.rem(c, 2)], ar.at[c], {'m2': jp[1]})

    def send_b(c):
        return rcopy(ss.at[lax.rem(c, 2)], rb.at[c], bs.at[lax.rem(c, 2)], br.at[c], {'m2': jp[2]})

    def send_c(c, k):
        src = rb.at[c, :, ds(ip[1 + 2 * k] * LANES, LANES)]
        return rcopy(src, rc.at[c, k], cs.at[0], cr.at[c], {'m1': ip[1]})

    def send_d(c):
        return rcopy(ud.at[c], rd.at[c], dsm.at[0], drm.at[c], {'m1': ip[2]})

    def out_part(c, q):
        return out.at[rows_at(q * rows, rows), ds(c * LANES, LANES)]

    def result(c, q, sem, recv, device):
        part = out_part(c, q)
        return rcopy(part, part, es.at[sem], recv, device)

    def product2(c):
        slot = lax.rem(c, 2)
        cols, to = ds(c * LANES, LANES), ds(i * LANES, LANES)
        loads = [pltpu.make_async_copy(wo.at[rows_at(i * qw, qw), cols], w2b.at[slot, 0:qw, to], w2b_sem.at[0]),
                 pltpu.make_async_copy(wd.at[rows_at(i * uw, uw), cols], w2b.at[slot, qw:qw + uw, to], w2b_sem.at[1])]
        for load in loads:
            load.start()
        part = w2.at[c, 0, :, 0:3 * LANES]
        rcopy(part, part, f2s.at[0], f2r.at[c], {'dp': 1 - g}).wait_recv()
        for e in (1, 2, 3):
            to = ds(ip[e] * LANES, LANES)
            for k in range(2):
                sems = 2 + 4 * (e - 1) + 2 * k
                loads.append(pltpu.make_async_copy(w2.at[c, k, 0:qh, to], w2b.at[slot, k * qh:(k + 1) * qh, to], w2b_sem.at[sems]))
                loads.append(pltpu.make_async_copy(w2.at[c, k, qh:qh + uh, to], w2b.at[slot, qw + k * uh:qw + (k + 1) * uh, to], w2b_sem.at[sems + 1]))
        for load in loads[2:]:
            load.start()

        @pl.when(c >= 2)
        def _():
            all_a(c - 2).wait_send()
        for load in loads:
            load.wait()
        for yy in range(2):
            for sub in range(2):
                at = rows_at(quarter(yy, 1 - jc) + sub * block, block)
                pa[slot, yy, sub * block:(sub + 1) * block, :] = dot(h[at, :], w2b[slot]).astype(jnp.bfloat16)
            send_a(c, yy).start()
        keep = lax.rem(c, 3)
        for yy in range(2):
            for sub in range(2):
                at = rows_at(quarter(yy, jc) + sub * block, block)
                po[keep, yy, sub * block:(sub + 1) * block, :] = dot(h[at, :], w2b[slot]).astype(jnp.bfloat16)

    def add(a, b):
        return (a.astype(jnp.float32) + b.astype(jnp.float32)).astype(jnp.bfloat16)

    def sum_core(d):
        keep = lax.rem(d, 3)
        rcopy(ra.at[d], ra.at[d], as_.at[0], ar.at[d], {'m2': jp[1]}).wait_recv()
        load = pltpu.make_async_copy(ra.at[d], rav, rav_sem.at[0])
        load.start()

        @pl.when(d >= 2)
        def _():
            send_b(d - 2).wait_send()
        load.wait()
        ss[lax.rem(d, 2)] = add(po[keep, 1 - jy], rav[1 - jy])
        send_b(d).start()
        po[keep, jy] = add(po[keep, jy], rav[jy])

    def sum_y(d):
        rcopy(rb.at[d], rb.at[d], bs.at[0], br.at[d], {'m2': jp[2]}).wait_recv()
        rb[d] = add(po[lax.rem(d, 3), jy], rb[d])
        for k in range(2):
            send_c(d, k).start()

    def sum_near(d):
        rcopy(rc.at[d], rc.at[d], cs.at[0], cr.at[d], {'m1': ip[1]}).wait_recv()
        ud[d] = add(rb[d, :, ds(ip[2] * LANES, LANES)], rc[d, 1])
        send_d(d).start()

    def finish(d):
        rcopy(rd.at[d], rd.at[d], dsm.at[0], drm.at[d], {'m1': ip[2]}).wait_recv()
        cols = ds(d * LANES, LANES)
        value = rb[d, :, ds(i * LANES, LANES)].astype(jnp.float32) + rc[d, 0].astype(jnp.float32) + rd[d].astype(jnp.float32)
        value = xg[i, :, cols].astype(jnp.float32) + value + bo[cols][None, :]
        out[rows_at(j * rows, rows), cols] = value.astype(jnp.bfloat16)
        result(d, j, 0, er.at[d], {'m2': jp[2]}).start()
        result(d, j, 1, fr.at[0], {'m2': jp[1]}).start()

    def pass_on(d):
        result(d, jp[2], 0, er.at[d], {'m2': jp[2]}).wait_recv()
        result(d, jp[2], 2, fr.at[1], {'m2': jp[1]}).start()

    def run(step, first, last):
        @pl.loop(first, last)
        def _(d):
            step(d)

    early = 2 + 2 * mid

    def late(c, lag, step, last=nc):
        @pl.when((c >= lag) & (c < last))
        def _():
            step(c - lag)

    @pl.loop(0, nc)
    def _(c):
        late(c, 2, sum_y)
        late(c, 1, sum_core)

        @pl.when((c >= 1) & (c + 1 < nc))
        def _():
            next2(c + 1)

        @pl.when(c == nc - 2)
        def _():
            run(sum_near, 0, early)

        @pl.when(c == nc - 1)
        def _():
            run(sum_near, early, early + 2)
            finish(0)
        product2(c)

    sum_core(nc - 1)
    run(sum_near, early + 2, early + 5)
    sum_y(nc - 2)
    run(sum_near, early + 5, nc - 2)
    run(finish, 1, 4)
    sum_y(nc - 1)
    sum_near(nc - 2)
    run(finish, 4, nc - 3)
    sum_near(nc - 1)
    run(finish, nc - 3, nc)
    run(pass_on, 0, nc)

    for copy in (x_far, x_near, x_fwd, u_far, u_near, u_fwd):
      copy.wait_send()
    for sem in (w1s, f1s):
        part = w1.at[:, 0:3 * half, :]
        rcopy(part, part, sem.at[0], w1r.at[0, 0], {'dp': 1 - g}).wait_send()
    for sem in (w2s, f2s):
        part = w2.at[:, 0, :, 0:3 * LANES]
        rcopy(part, part, sem.at[0], f2r.at[0], {'dp': 1 - g}).wait_send()
    for c in (nc - 2, nc - 1):
        all_a(c).wait_send()
        send_b(c).wait_send()
    rcopy(rc, rc, cs.at[0], cr.at[0], {'m1': ip[1]}).wait_send()
    for sem in (dsm.at[0], es.at[0], es.at[1], es.at[2]):
        rcopy(rd, rd, sem, drm.at[0], {'m1': ip[2]}).wait_send()
    for k in range(2):
        rcopy(rd, rd, es.at[1], fr.at[k], {'m2': jp[1]}).wait_recv()


def solution(mesh):
    assert mesh.shape['m1'] == 4 and mesh.shape['m2'] == 4 and mesh.shape['dp'] == 2

    def local_layer(x_blk, ln_scale, qn_scale, kn_scale, w_qkv, w_up, b_up, w_o, w_down, b_out):
        batch, patches, dim = x_blk.shape
        tokens = batch * patches
        qw, uw = w_qkv.shape[2] // 4, w_up.shape[1] // 4
        rows, block, nc, nb = tokens // 4, tokens // 8, dim // LANES, 3 + uw // qw
        assert qn_scale.shape[0] == LANES and uw % qw == 0 and nb == 7
        wide = 4 * LANES
        bf16 = jnp.bfloat16
        dma = pltpu.SemaphoreType.DMA
        hbm = pl.BlockSpec(memory_space=pltpu.HBM)
        vmem = pl.BlockSpec(memory_space=pltpu.VMEM)
        ln_rows = min(64, rows)
        out = pl.pallas_call(
            functools.partial(kernel, (batch, patches, dim, qw, uw)),
            out_shape=[
                pltpu.VMEM((tokens, dim), bf16),
                jax.ShapeDtypeStruct((tokens, 4 * dim), bf16),
                jax.ShapeDtypeStruct((nb, 4 * dim, qw), bf16),
                jax.ShapeDtypeStruct((nc, 2, (qw + uw) // 2, wide), bf16),
                jax.ShapeDtypeStruct((nc, 2, rows, wide), bf16)],
            in_specs=[hbm, vmem, vmem, vmem, hbm, hbm, vmem, hbm, hbm, vmem],
            out_specs=[vmem] + [hbm] * 4,
            scratch_shapes=[
                pltpu.VMEM((4, rows, dim), bf16),
                pltpu.VMEM((2, ln_rows, 4 * dim), bf16),
                pltpu.VMEM((3, tokens, qw), bf16),
                pltpu.VMEM((tokens, qw + uw), bf16),
                pltpu.VMEM((4 * dim, qw), bf16),
                pltpu.VMEM((2, block, 4 * dim), bf16),
                pltpu.VMEM((2, qw + uw, wide), bf16),
                pltpu.VMEM((2, 2, rows, wide), bf16),
                pltpu.VMEM((3, 2, rows, wide), bf16),
                pltpu.VMEM((2, rows, wide), bf16),
                pltpu.VMEM((2, rows, wide), bf16),
                pltpu.VMEM((nc, rows, wide), bf16),
                pltpu.VMEM((nc, 2, rows, LANES), bf16),
                pltpu.VMEM((nc, rows, LANES), bf16),
                pltpu.VMEM((nc, rows, LANES), bf16),
                dma((3,)), dma((3,)),
                dma((1,)), dma((nb, 3)), dma((1,)), dma((nb,)),
                dma((3,)), dma((3,)),
                dma((1,)), dma((nc, 3)), dma((1,)), dma((nc,)),
                dma((2,)), dma((nc,)), dma((2,)), dma((nc,)), dma((1,)), dma((nc,)), dma((1,)), dma((nc,)),
                dma((3,)), dma((nc,)), dma((2,)),
                dma((1,)), dma((4,)), dma((2,)), dma((2,)), dma((14,)), dma((1,))],
            compiler_params=pltpu.CompilerParams(collective_id=0, has_side_effects=True, vmem_limit_bytes=60_000_000),
            name='layer',
        )(x_blk.reshape(tokens, dim), ln_scale[None], qn_scale[None], kn_scale[None], w_qkv.transpose(1, 0, 2), w_up,
          b_up[None], w_o, w_down, b_out)[0]
        return out.reshape(batch, patches, dim)

    return jax.shard_map(local_layer, mesh=mesh, in_specs=(P('dp', None, 'm1'), P(), P(), P(), P('m1', None, 'm2'), P('m1', 'm2'), P('m2'), P('m2', 'm1'), P('m2', 'm1'), P('m1')), out_specs=P('dp', None, 'm1'), check_vma=False)
```

profile of v0, /device:TPU:0, one launch (start us, length us, event | category | flops | bytes accessed | tf_op | source)
XLA Modules:
  0.0 761.1 jit_solution(8226959365986996514)
XLA Ops:
  0.0 758.4 %layer.1 = (bf16[2048,1536]{1,0:T(8,128)(2,1)S(1)}, bf16[2048,6144]{1,0:T(8,128)(2,1)}, bf16[7,6144,384]{2,1,0:T(8,128)(2,1)}, bf16[12,2,960,512]{3,2,1,0:T(8,128)(2,1)}, bf16[12,2,512,512]{3,2,1,0:T(8,128)(2,1)}) custom-call(bf16[2048,1536]{1,0:T(8,128)(2,1)} %bitcast.9, f32[1,6144]{1,0:T(1,128)} %bitcast.10, f32[1,128]{1,0:T(1,128)} %bitcast.12, ...), custom_call_target="tpu_custom_call" | custom-call | tf_op jit(solution)/shard_map/layer/pallas_call | solution.py:434
  758.4 2.7 copy.12
where the time goes:
time: 764 us; the launch traced here: 761 us
  Pallas kernels  758 us (99%)
    pallas_call x1, Pallas kernels, local_layer(): pl.pallas_call(functools.partial(kernel, (batch, patches, dim, qw, uw)),...  758 us

commit v1 on v0

--- a/solution.py
+++ b/solution.py
@@ -284,7 +284,7 @@
         slot = lax.rem(c, 2)
         cols, to = ds(c * LANES, LANES), ds(i * LANES, LANES)
         loads = [pltpu.make_async_copy(wo.at[rows_at(i * qw, qw), cols], w2b.at[slot, 0:qw, to], w2b_sem.at[0]),
-                 pltpu.make_async_copy(wd.at[rows_at(i * uw, uw), cols], w2b.at[slot, qw:qw + uw, to], w2b_sem.at[1])]
+                 pltpu.make_async_copy(wd.at[rows_at(i * uw, uw), cols], w2b.at[slot, qw:qw + uw, to], w2b_sem.at[0])]
         for load in loads:
             load.start()
         part = w2.at[c, 0, :, 0:3 * LANES]
@@ -292,17 +292,15 @@
         for e in (1, 2, 3):
             to = ds(ip[e] * LANES, LANES)
             for k in range(2):
-                sems = 2 + 4 * (e - 1) + 2 * k
-                loads.append(pltpu.make_async_copy(w2.at[c, k, 0:qh, to], w2b.at[slot, k * qh:(k + 1) * qh, to], w2b_sem.at[sems]))
-                loads.append(pltpu.make_async_copy(w2.at[c, k, qh:qh + uh, to], w2b.at[slot, qw + k * uh:qw + (k + 1) * uh, to], w2b_sem.at[sems + 1]))
+                loads.append(pltpu.make_async_copy(w2.at[c, k, 0:qh, to], w2b.at[slot, k * qh:(k + 1) * qh, to], w2b_sem.at[0]))
+                loads.append(pltpu.make_async_copy(w2.at[c, k, qh:qh + uh, to], w2b.at[slot, qw + k * uh:qw + (k + 1) * uh, to], w2b_sem.at[0]))
         for load in loads[2:]:
             load.start()
 
         @pl.when(c >= 2)
         def _():
             all_a(c - 2).wait_send()
-        for load in loads:
-            load.wait()
+        pltpu.make_async_copy(w2b.at[1 - slot], w2b.at[slot], w2b_sem.at[0]).wait()
         for yy in range(2):
             for sub in range(2):
                 at = rows_at(quarter(yy, 1 - jc) + sub * block, block)
@@ -372,11 +370,15 @@
         late(c, 2, sum_y)
         late(c, 1, sum_core)
 
+        @pl.when((c == nc - 2) & (mid == 1))
+        def _():
+            run(sum_near, 0, early)
+
         @pl.when((c >= 1) & (c + 1 < nc))
         def _():
             next2(c + 1)
 
-        @pl.when(c == nc - 2)
+        @pl.when((c == nc - 2) & (mid == 0))
         def _():
             run(sum_near, 0, early)
 
@@ -393,9 +395,10 @@
     run(finish, 1, 4)
     sum_y(nc - 1)
     sum_near(nc - 2)
-    run(finish, 4, nc - 3)
+    ready = nc // 2 + 3 * mid
+    run(finish, 4, ready)
     sum_near(nc - 1)
-    run(finish, nc - 3, nc)
+    run(finish, ready, nc)
     run(pass_on, 0, nc)
 
     for copy in (x_far, x_near, x_fwd, u_far, u_near, u_fwd):
@@ -463,7 +466,7 @@
                 dma((1,)), dma((nc, 3)), dma((1,)), dma((nc,)),
                 dma((2,)), dma((nc,)), dma((2,)), dma((nc,)), dma((1,)), dma((nc,)), dma((1,)), dma((nc,)),
                 dma((3,)), dma((nc,)), dma((2,)),
-                dma((1,)), dma((4,)), dma((2,)), dma((2,)), dma((14,)), dma((1,))],
+                dma((1,)), dma((4,)), dma((2,)), dma((2,)), dma((1,)), dma((1,))],
             compiler_params=pltpu.CompilerParams(collective_id=0, has_side_effects=True, vmem_limit_bytes=60_000_000),
             name='layer',
         )(x_blk.reshape(tokens, dim), ln_scale[None], qn_scale[None], kn_scale[None], w_qkv.transpose(1, 0, 2), w_up,

time: 764 us -> 764 us (level)
  no operation moved by 1% of the time
where the time goes in v1:
time: 764 us; the launch traced here: 761 us
  Pallas kernels  759 us (99%)
    pallas_call x1, Pallas kernels, local_layer(): pl.pallas_call(functools.partial(kernel, (batch, patches, dim, qw, uw)),...  759 us

profile of v1, /device:TPU:0, one launch (start us, length us, event | category | flops | bytes accessed | tf_op | source)
XLA Modules:
  0.0 761.2 jit_solution(17123749843563401519)
XLA Ops:
  0.0 758.5 %layer.1 = (bf16[2048,1536]{1,0:T(8,128)(2,1)S(1)}, bf16[2048,6144]{1,0:T(8,128)(2,1)}, bf16[7,6144,384]{2,1,0:T(8,128)(2,1)}, bf16[12,2,960,512]{3,2,1,0:T(8,128)(2,1)}, bf16[12,2,512,512]{3,2,1,0:T(8,128)(2,1)}) custom-call(bf16[2048,1536]{1,0:T(8,128)(2,1)} %bitcast.9, f32[1,6144]{1,0:T(1,128)} %bitcast.10, f32[1,128]{1,0:T(1,128)} %bitcast.12, ...), custom_call_target="tpu_custom_call" | custom-call | tf_op jit(solution)/shard_map/layer/pallas_call | solution.py:437
  758.5 2.7 copy.12

commit v2 on v0

--- a/solution.py
+++ b/solution.py
@@ -360,7 +360,7 @@
         def _(d):
             step(d)
 
-    early = 2 + 2 * mid
+    early = 1 + 3 * mid
 
     def late(c, lag, step, last=nc):
         @pl.when((c >= lag) & (c < last))

time: 764 us -> 765 us (level)
  no operation moved by 1% of the time
where the time goes in v2:
time: 765 us; the launch traced here: 762 us
  Pallas kernels  759 us (99%)
    pallas_call x1, Pallas kernels, local_layer(): pl.pallas_call(functools.partial(kernel, (batch, patches, dim, qw, uw)),...  759 us

profile of v2, /device:TPU:0, one launch (start us, length us, event | category | flops | bytes accessed | tf_op | source)
XLA Modules:
  0.0 762.1 jit_solution(8693816412094734790)
XLA Ops:
  0.0 759.4 %layer.1 = (bf16[2048,1536]{1,0:T(8,128)(2,1)S(1)}, bf16[2048,6144]{1,0:T(8,128)(2,1)}, bf16[7,6144,384]{2,1,0:T(8,128)(2,1)}, bf16[12,2,960,512]{3,2,1,0:T(8,128)(2,1)}, bf16[12,2,512,512]{3,2,1,0:T(8,128)(2,1)}) custom-call(bf16[2048,1536]{1,0:T(8,128)(2,1)} %bitcast.9, f32[1,6144]{1,0:T(1,128)} %bitcast.10, f32[1,128]{1,0:T(1,128)} %bitcast.12, ...), custom_call_target="tpu_custom_call" | custom-call | tf_op jit(solution)/shard_map/layer/pallas_call | solution.py:434
  759.4 2.7 copy.12

commit v3 on v2

--- a/solution.py
+++ b/solution.py
@@ -360,7 +360,7 @@
         def _(d):
             step(d)
 
-    early = 1 + 3 * mid
+    early = 2 + mid
 
     def late(c, lag, step, last=nc):
         @pl.when((c >= lag) & (c < last))

time: 765 us -> 764 us (level)
  no operation moved by 1% of the time
where the time goes in v3:
time: 764 us; the launch traced here: 761 us
  Pallas kernels  759 us (99%)
    pallas_call x1, Pallas kernels, local_layer(): pl.pallas_call(functools.partial(kernel, (batch, patches, dim, qw, uw)),...  759 us

profile of v3, /device:TPU:0, one launch (start us, length us, event | category | flops | bytes accessed | tf_op | source)
XLA Modules:
  0.0 761.2 jit_solution(10488944599259916106)
XLA Ops:
  0.0 758.5 %layer.1 = (bf16[2048,1536]{1,0:T(8,128)(2,1)S(1)}, bf16[2048,6144]{1,0:T(8,128)(2,1)}, bf16[7,6144,384]{2,1,0:T(8,128)(2,1)}, bf16[12,2,960,512]{3,2,1,0:T(8,128)(2,1)}, bf16[12,2,512,512]{3,2,1,0:T(8,128)(2,1)}) custom-call(bf16[2048,1536]{1,0:T(8,128)(2,1)} %bitcast.9, f32[1,6144]{1,0:T(1,128)} %bitcast.10, f32[1,128]{1,0:T(1,128)} %bitcast.12, ...), custom_call_target="tpu_custom_call" | custom-call | tf_op jit(solution)/shard_map/layer/pallas_call | solution.py:434
  758.5 2.7 copy.12

commit v4 on v0

--- a/solution.py
+++ b/solution.py
@@ -10,7 +10,7 @@
 LN_EPS = 1e-6
 MESH = pl.DeviceIdType.MESH
 LANES = 128
-AHEAD = 2
+AHEAD = 3
 
 
 def xors(value):

time: 764 us -> 767 us (level)
  no operation moved by 1% of the time
where the time goes in v4:
time: 767 us; the launch traced here: 763 us
  Pallas kernels  761 us (99%)
    pallas_call x1, Pallas kernels, local_layer(): pl.pallas_call(functools.partial(kernel, (batch, patches, dim, qw, uw)),...  761 us

profile of v4, /device:TPU:0, one launch (start us, length us, event | category | flops | bytes accessed | tf_op | source)
XLA Modules:
  0.0 763.2 jit_solution(16493275744460006780)
XLA Ops:
  0.0 760.5 %layer.1 = (bf16[2048,1536]{1,0:T(8,128)(2,1)S(1)}, bf16[2048,6144]{1,0:T(8,128)(2,1)}, bf16[7,6144,384]{2,1,0:T(8,128)(2,1)}, bf16[12,2,960,512]{3,2,1,0:T(8,128)(2,1)}, bf16[12,2,512,512]{3,2,1,0:T(8,128)(2,1)}) custom-call(bf16[2048,1536]{1,0:T(8,128)(2,1)} %bitcast.9, f32[1,6144]{1,0:T(1,128)} %bitcast.10, f32[1,128]{1,0:T(1,128)} %bitcast.12, ...), custom_call_target="tpu_custom_call" | custom-call | tf_op jit(solution)/shard_map/layer/pallas_call | solution.py:434
  760.5 2.7 copy.12
